TPU v7x, 256 devices: a 4x2x16 block of a 4x16x16 slice. The times are simulated.
256 devices in a mesh: groups: 2 (over y), tp: 16 (over z), tq: 4 (over x), tr: 2 (over core).
Axes of the slice: x: 4, y: 2, z: 16, core: 2. Of those that a mesh axis runs over, the one named last changes fastest.
The devices are a block of a 4x16x16 slice.
Arguments:
- attn_heads: bfloat16 [128, 16384], P('groups', ('tp', 'tq', 'tr')), parts along dimension 0, may hold values from -6 to 6
- residual: bfloat16 [128, 16384], P('groups', ('tp', 'tq', 'tr')), parts along dimension 0, may hold values from -120 to 120
- o_weight: bfloat16 [16384, 16384], P(('tp', 'tq', 'tr')), may hold values from -0.1875 to 0.1875
- norm_gain: bfloat16 [16384], P(('tp', 'tq', 'tr')), may hold values from 0.099609375 to 1.8984375
- q_weight: bfloat16 [16384, 16384], P(None, ('tp', 'tq', 'tr')), may hold values from -0.046875 to 0.046875
Outputs:
- hidden: bfloat16 [128, 16384], P('groups', ('tp', 'tq', 'tr')), parts along dimension 0
- peak_value: float32 [128], P('groups'), parts along dimension 0
- query: bfloat16 [128, 16384], P('groups', ('tp', 'tq', 'tr')), parts along dimension 0
There are 2 independent parts, one for each index of `groups`. A program takes and returns all parts, laid end to end along the dimension named above; an argument that names none is the same for every part. Nothing has to cross between parts.
All inputs are finite; a program needn't handle non-finite values. Where the computation divides by a largest or mean magnitude, that divisor is 1e-20 or more.
Results may differ from a plain program's by a relative error of at most 0.0095.
Values may be sent and summed in bfloat16 or wider, within the bound.
No kernel may reach another device: no remote copies, remote signals or barrier semaphores. Data moves between devices by JAX's collectives and lax.ppermute only.
A program may use at most 64 MiB of HBM per device.

v0:
```python
import jax
import jax.numpy as jnp
from jax import lax
from jax.sharding import PartitionSpec as P

D = 16384


def in_blocks(array, dim, devices):
    dims = array.shape
    tiles = array.reshape(*dims[:dim], devices, dims[dim] // devices, *dims[dim + 1 :])
    return jnp.moveaxis(tiles, dim, 0)


def summed_on_arrival(array, axis, dim):
    tiles = in_blocks(array, dim, lax.axis_size(axis))
    arrived = lax.all_to_all(tiles, axis, split_axis=0, concat_axis=0, tiled=True)
    return arrived.sum(axis=0)


def collected_together(array, axis):
    leaves = jax.tree.leaves(array)
    turns = sorted(range(len(leaves)), key=lambda k: -leaves[k].size)
    width = (1, *leaves[turns[0]].shape)[-1]
    lines = [
        jnp.pad(leaves[k].reshape(-1), (0, -leaves[k].size % width)).reshape(-1, width)
        for k in turns
    ]
    both, at, found = (lax.all_gather(jnp.concatenate(lines), axis), 0, {})
    for k, line in zip(turns, lines):
        share = both[:, at : at + len(line)].reshape(len(both), -1)
        found[k] = share[:, : leaves[k].size].reshape(-1, *leaves[k].shape)
        at += len(line)
    numbers = iter(range(len(leaves)))
    return jax.tree.map(lambda _: found[next(numbers)], array)


def joined_all(array, axes, combine):
    for axis in axes:
        pieces = collected_together(array, axis)
        array = jax.tree.map(lambda part: part[0], pieces)
        for k in range(1, lax.axis_size(axis)):
            array = combine(array, jax.tree.map(lambda part: part[k], pieces))
    return array


def laid_out(tiles, dim):
    tiles = jnp.moveaxis(tiles, 0, dim)
    dims = tiles.shape
    return tiles.reshape(*dims[:dim], dims[dim] * dims[dim + 1], *dims[dim + 2 :])


def from_everyone(array, axis):
    copies = jnp.broadcast_to(array, (lax.axis_size(axis), *array.shape))
    return lax.all_to_all(copies, axis, split_axis=0, concat_axis=0, tiled=True)


def collect(array, axis, dim):
    return laid_out(from_everyone(array, axis), dim)


def combine_stats(lhs_stats, rhs_stats):
    return (lhs_stats[0] + rhs_stats[0], jnp.maximum(lhs_stats[1], rhs_stats[1]))


def body(attn_heads, residual, o_weight, norm_gain, q_weight):
    terms = jnp.dot(attn_heads, o_weight, preferred_element_type=jnp.float32)
    section_one = lax.psum_scatter(terms, "tp", scatter_dimension=1, tiled=True)
    section_two = summed_on_arrival(section_one, "tq", 1)
    attn_total = summed_on_arrival(section_two, "tr", 1)
    hidden = (residual.astype(jnp.float32) + attn_total).astype(jnp.bfloat16)
    widened = hidden.astype(jnp.float32)
    gained = widened * norm_gain.astype(jnp.float32)
    squares = jnp.sum(widened * widened, axis=1)
    local_top = jnp.max(jnp.abs(gained), axis=1)
    row_total, global_top = joined_all((squares, local_top), ("tp", "tq", "tr"), combine_stats)
    inv_rms = lax.rsqrt(row_total / D + 1e-05)
    normed = gained * inv_rms[:, None]
    peak_value = global_top * inv_rms
    quantized = (normed * (448.0 / (peak_value + 1e-06))[:, None]).astype(jnp.bfloat16)
    gathered_two = collect(quantized, "tr", 1)
    gathered_four = collect(gathered_two, "tq", 1)
    projected = jnp.dot(
        lax.all_gather(gathered_four, "tp", axis=1, tiled=True),
        q_weight,
        preferred_element_type=jnp.float32,
    )
    query = (projected * ((peak_value + 1e-06) / 448.0)[:, None]).astype(jnp.bfloat16)
    return (hidden, peak_value, query)


def solution(mesh):
    placed = (
        P("groups", ("tp", "tq", "tr")),
        P("groups", ("tp", "tq", "tr")),
        P(("tp", "tq", "tr"), None),
        P(("tp", "tq", "tr")),
        P(None, ("tp", "tq", "tr")),
    )
    return jax.shard_map(
        body,
        mesh=mesh,
        in_specs=placed,
        out_specs=(P("groups", ("tp", "tq", "tr")), P("groups"), P("groups", ("tp", "tq", "tr"))),
        check_vma=False,
    )
```

profile of v0, /device:TPU:34, one launch (start us, length us, event | category | flops | bytes accessed | tf_op | source)
XLA Modules:
  0.0 252.2 jit_solution(817903353825983854)
XLA Ops:
  7.2 0.0 copy-start
  7.2 0.1 reduce-scatter.2.cloned.1.call-start
  7.3 0.6 copy-done
  7.9 4.8 %fusion.15 = f32[64,16384]{1,0:T(8,128)} fusion(bf16[64,128]{1,0:T(8,128)(2,1)S(1)} %copy-done, bf16[128,16384]{1,0:T(8,128)(2,1)} %param.7), kind=kOutput, calls=%fused_computation.64 | convolution fusion | flops 268435456 | bytes 8404992 | tf_op jit(solution)/shard_map/dot_general | solution.py:67
  12.7 0.0 copy-start.4
  12.7 0.0 copy-start.2
  12.7 0.1 reduce-scatter.2.cloned.1.call-update
  12.8 92.7 %reduce-scatter.2.cloned.1.call-done = f32[64,1024]{1,0:T(8,128)} async-done(((f32[64,16384]{1,0:T(8,128)}), f32[64,1024]{1,0:T(8,128)}) %reduce-scatter.2.cloned.1.call-update) | async-done | bytes 262160 | tf_op jit(solution)/shard_map/reduce_scatter | solution.py:68
  105.5 1.7 copy.20
  107.1 5.0 %all-to-all-start = ((f32[4,64,256]{2,1,0:T(8,128)}), f32[4,64,256]{2,1,0:T(8,128)S(1)}, u32[]{:S(2)}, u32[]{:S(2)}) async-start(f32[4,64,256]{2,1,0:T(8,128)} %bitcast.44), calls=%async_computation.1 | async-start | bytes 524288 | tf_op jit(solution)/shard_map/all_to_all | solution.py:17
  112.2 0.0 all-gather.8.cloned.1.call-start
  112.2 0.0 copy-done.4
  112.2 5.2 %all-to-all-done = f32[4,64,256]{2,1,0:T(8,128)S(1)} async-done(((f32[4,64,256]{2,1,0:T(8,128)}), f32[4,64,256]{2,1,0:T(8,128)S(1)}, u32[]{:S(2)}, u32[]{:S(2)}) %all-to-all-start) | async-done | bytes 262176 | tf_op jit(solution)/shard_map/all_to_all | solution.py:17
  117.5 3.8 %all_to_all.20 = f32[2,64,128]{2,1,0:T(8,128)S(1)} all-to-all(f32[2,64,128]{2,1,0:T(8,128)S(1)} %copy.12), channel_id=1, replica_groups=mesh['groups'=2,'tp'=16,'tq'=4,'tr'=2] {'tr'}, dimensions={0} | all-to-all | bytes 131072 | tf_op jit(solution)/shard_map/all_to_all | solution.py:17
  121.3 0.0 copy-done.2
  121.3 0.1 fusion.6
  121.4 0.0 copy-start.1
  121.4 27.3 %all-gather.3 = f32[16,2,64]{2,1,0:T(2,128)S(1)} all-gather(f32[1,2,64]{2,1,0:T(2,128)S(1)} %maximum_bitcast_fusion), channel_id=2, replica_groups=mesh['groups'=2,'tp'=16,'tq'=4,'tr'=2] {'tp'}, dimensions={0}, use_global_device_ids=true | all-gather | bytes 8704 | tf_op jit(solution)/shard_map/all_gather | solution.py:29
  148.7 8.5 %all-gather.4 = f32[4,2,64]{2,1,0:T(2,128)S(1)} all-gather(f32[1,2,64]{2,1,0:T(2,128)S(1)} %maximum_bitcast_fusion.1), channel_id=3, replica_groups=mesh['groups'=2,'tp'=16,'tq'=4,'tr'=2] {'tq'}, dimensions={0}, use_global_device_ids=true | all-gather | bytes 2560 | tf_op jit(solution)/shard_map/all_gather | solution.py:29
  157.3 1.9 all-gather.5
  159.1 0.0 copy-start.3
  159.2 0.1 fusion.5
  159.3 3.8 %all_to_all.21 = bf16[2,64,128]{2,1,0:T(8,128)(2,1)S(1)} all-to-all(bf16[2,64,128]{2,1,0:T(8,128)(2,1)S(1)} %broadcast_in_dim.4), channel_id=1, replica_groups=mesh['groups'=2,'tp'=16,'tq'=4,'tr'=2] {'tr'}, dimensions={0} | all-to-all | bytes 65536 | tf_op jit(solution)/shard_map/all_to_all | solution.py:55
  163.0 8.1 %all_to_all.22 = bf16[4,64,256]{2,1,0:T(8,128)(2,1)S(1)} all-to-all(bf16[4,64,256]{2,1,0:T(8,128)(2,1)S(1)} %broadcast_in_dim.5), channel_id=1, replica_groups=mesh['groups'=2,'tp'=16,'tq'=4,'tr'=2] {'tq'}, dimensions={0} | all-to-all | bytes 262144 | tf_op jit(solution)/shard_map/all_to_all | solution.py:55
  171.1 0.7 copy.17
  171.8 0.1 all-gather.8.cloned.1.call-update
  171.9 69.2 %all-gather.8.cloned.1.call-done = bf16[64,16384]{1,0:T(8,128)(2,1)} async-done(((bf16[64,1024]{1,0:T(8,128)(2,1)}), bf16[64,16384]{1,0:T(8,128)(2,1)}) %all-gather.8.cloned.1.call-update) | async-done | bytes 2097168 | tf_op jit(solution)/shard_map/all_gather | solution.py:84
  241.1 4.3 %fusion = bf16[64,128]{1,0:T(8,128)(2,1)} fusion(bf16[64,16384]{1,0:T(8,128)(2,1)} %all-gather.8.cloned.1.call-done, bf16[16384,128]{1,0:T(8,128)(2,1)} %param.9, f32[64]{0:T(128)S(1)} %get-tuple-element.5), kind=kOutput, calls=%fused_computation.1 | convolution fusion | flops 268451840 | bytes 6308096 | tf_op jit(solution)/shard_map/dot_general | solution.py:83
  245.3 0.0 copy-done.1
  245.3 0.0 copy-done.3
  (16 shorter events, 0.2 us)
Async XLA Ops:
  7.2 0.7 copy-start
  7.2 98.3 %reduce-scatter.2.cloned.1.call-start = ((), (), s32[]{:S(2)}) async-start(), calls=%async_computation.5 | async-start | bytes 4456448 | tf_op jit(solution)/shard_map/reduce_scatter | solution.py:68
  12.7 99.4 %copy-start.4 = (bf16[128]{0:T(256)(128)(2,1)S(1)}, bf16[128]{0:T(256)(128)(2,1)}, u32[]{:S(2)}) copy-start(bf16[128]{0:T(256)(128)(2,1)} %param.8) | copy-start | bytes 772
  12.7 108.5 %copy-start.2 = (bf16[64,128]{1,0:T(8,128)(2,1)S(1)}, bf16[64,128]{1,0:T(8,128)(2,1)}, u32[]{:S(2)}) copy-start(bf16[64,128]{1,0:T(8,128)(2,1)} %param.6) | copy-start | bytes 49156
  107.1 10.3 %all-to-all-start = ((f32[4,64,256]{2,1,0:T(8,128)}), f32[4,64,256]{2,1,0:T(8,128)S(1)}, u32[]{:S(2)}, u32[]{:S(2)}) async-start(f32[4,64,256]{2,1,0:T(8,128)} %bitcast.44), calls=%async_computation.1 | async-start | bytes 524288 | tf_op jit(solution)/shard_map/all_to_all | solution.py:17
  112.2 128.9 %all-gather.8.cloned.1.call-start = ((), (), s32[]{:S(2)}) async-start(), calls=%async_computation.6 | async-start | bytes 2228224 | tf_op jit(solution)/shard_map/all_gather | solution.py:84
  121.4 124.0 %copy-start.1 = (bf16[64,128]{1,0:T(8,128)(2,1)}, bf16[64,128]{1,0:T(8,128)(2,1)S(1)}, u32[]{:S(2)}) copy-start(bf16[64,128]{1,0:T(8,128)(2,1)S(1)} %get-tuple-element.8) | copy-start | bytes 49156
  159.1 86.2 %copy-start.3 = (f32[64]{0:T(128)}, f32[64]{0:T(128)S(1)}, u32[]{:S(2)}) copy-start(f32[64]{0:T(128)S(1)} %get-tuple-element.6) | copy-start | bytes 772
Sparse Core Ops, SparseCore 0:
  12.9 92.5 reduce-scatter.1
  172.0 69.0 all-gather.7
where the time goes:
time: 253 us; the launch traced here: 252 us
  waiting for transfers between devices  167 us (66%)
  blocking collectives  53.3 us (21%)
  between operations  14.2 us (6%)
  matrix products  9.1 us (4%)
  starting transfers between devices  5.09 us (2%)
  local copies, waits for them, and re-layouts  3.06 us (1%)
    reduce_scatter x1, waiting for transfers between devices, body(): section_one = lax.psum_scatter(terms, 'tp', scatter_dimension=1, tiled=True)  92.7 us
    all_gather x1, waiting for transfers between devices, body(): lax.all_gather(gathered_four, 'tp', axis=1, tiled=True)  69.2 us
    all_gather x3, blocking collectives, collected_together(): both, at, found = (lax.all_gather(jnp.concatenate(lines), axis), 0, {})  37.6 us
    all_to_all x2, blocking collectives, from_everyone(): return lax.all_to_all(copies, axis, split_axis=0, concat_axis=0, tiled=True)  11.9 us
    all_to_all x1, waiting for transfers between devices, summed_on_arrival(): lax.all_to_all(tiles, axis, split_axis=0, concat_axis=0, tiled=True)  5.21 us
  transfers between devices with their start and end apart: 3, of which 3 were waited for; matrix products, arithmetic and copies ran while one was open for 0% of the time, Pallas kernels for 0%

commit v1 on v0

--- a/solution.py
+++ b/solution.py
@@ -4,6 +4,14 @@
 from jax.sharding import PartitionSpec as P
 
 D = 16384
+
+
+def gather_by_exchange(value, axis, dim):
+    count = lax.axis_size(axis)
+    repeats = [count if d == dim else 1 for d in range(value.ndim)]
+    return lax.all_to_all(
+        jnp.tile(value, repeats), axis, split_axis=dim, concat_axis=dim, tiled=True
+    )
 
 
 def in_blocks(array, dim, devices):
@@ -81,9 +89,7 @@
     gathered_two = collect(quantized, "tr", 1)
     gathered_four = collect(gathered_two, "tq", 1)
     projected = jnp.dot(
-        lax.all_gather(gathered_four, "tp", axis=1, tiled=True),
-        q_weight,
-        preferred_element_type=jnp.float32,
+        gather_by_exchange(gathered_four, "tp", 1), q_weight, preferred_element_type=jnp.float32
     )
     query = (projected * ((peak_value + 1e-06) / 448.0)[:, None]).astype(jnp.bfloat16)
     return (hidden, peak_value, query)

time: 253 us -> 286 us (1.13)
  blocking collectives: 53.3 us -> 159 us
  waiting for transfers between devices: 167 us -> 97.9 us
    all_to_all x0 -> x1, blocking collectives: none -> 106 us  [gather_by_exchange(): lax.all_to_all(jnp.tile(value, repeats), axis, split_axis=dim, concat_axi...]
    all_gather x1 -> x0, waiting for transfers between devices: 69.2 us -> none  [body(): lax.all_gather(gathered_four, 'tp', axis=1, tiled=True)]
  transfers between devices with their start and end apart: 3 -> 2, of which waited for: 3 -> 2; matrix products, arithmetic and copies ran while one was open for 0% -> 0% of each run, Pallas kernels for 0% -> 0%
where the time goes in v1:
time: 286 us
  blocking collectives  159 us (56%)
  waiting for transfers between devices  97.9 us (34%)
  between operations  14.2 us (5%)
  matrix products  6.28 us (2%)
  starting transfers between devices  5.09 us (2%)
  local copies, waits for them, and re-layouts  2.9 us (1%)
    all_to_all x1, blocking collectives, gather_by_exchange(): lax.all_to_all(jnp.tile(value, repeats), axis, split_axis=dim, concat_axi...  106 us
    reduce_scatter x1, waiting for transfers between devices, body(): section_one = lax.psum_scatter(terms, 'tp', scatter_dimension=1, tiled=True)  92.7 us
    all_gather x3, blocking collectives, collected_together(): both, at, found = (lax.all_gather(jnp.concatenate(lines), axis), 0, {})  37.6 us
    all_to_all x2, blocking collectives, from_everyone(): return lax.all_to_all(copies, axis, split_axis=0, concat_axis=0, tiled=True)  11.9 us
  transfers between devices with their start and end apart: 2, of which 2 were waited for; matrix products, arithmetic and copies ran while one was open for 0% of the time, Pallas kernels for 0%

profile of v1, /device:TPU:34, one launch (start us, length us, event | category | flops | bytes accessed | tf_op | source)
XLA Modules:
  0.0 285.6 jit_solution(1174764520111062832)
XLA Ops:
  7.2 0.0 copy-start
  7.2 0.1 reduce-scatter.2.cloned.1.call-start
  7.3 0.6 copy-done
  7.9 4.8 %fusion.15 = f32[64,16384]{1,0:T(8,128)} fusion(bf16[64,128]{1,0:T(8,128)(2,1)S(1)} %copy-done, bf16[128,16384]{1,0:T(8,128)(2,1)} %param.7), kind=kOutput, calls=%fused_computation.64 | convolution fusion | flops 268435456 | bytes 8404992 | tf_op jit(solution)/shard_map/dot_general | solution.py:75
  12.7 0.0 copy-start.5
  12.7 0.0 copy-start.3
  12.7 0.1 reduce-scatter.2.cloned.1.call-update
  12.8 92.7 %reduce-scatter.2.cloned.1.call-done = f32[64,1024]{1,0:T(8,128)} async-done(((f32[64,16384]{1,0:T(8,128)}), f32[64,1024]{1,0:T(8,128)}) %reduce-scatter.2.cloned.1.call-update) | async-done | bytes 262160 | tf_op jit(solution)/shard_map/reduce_scatter | solution.py:76
  105.5 1.7 copy.22
  107.1 5.0 %all-to-all-start = ((f32[4,64,256]{2,1,0:T(8,128)}), f32[4,64,256]{2,1,0:T(8,128)S(1)}, u32[]{:S(2)}, u32[]{:S(2)}) async-start(f32[4,64,256]{2,1,0:T(8,128)} %bitcast.46), calls=%async_computation.1 | async-start | bytes 524288 | tf_op jit(solution)/shard_map/all_to_all | solution.py:25
  112.1 0.0 copy-done.5
  112.2 5.2 %all-to-all-done = f32[4,64,256]{2,1,0:T(8,128)S(1)} async-done(((f32[4,64,256]{2,1,0:T(8,128)}), f32[4,64,256]{2,1,0:T(8,128)S(1)}, u32[]{:S(2)}, u32[]{:S(2)}) %all-to-all-start) | async-done | bytes 262176 | tf_op jit(solution)/shard_map/all_to_all | solution.py:25
  117.4 3.8 %all_to_all.29 = f32[2,64,128]{2,1,0:T(8,128)S(1)} all-to-all(f32[2,64,128]{2,1,0:T(8,128)S(1)} %copy.12), channel_id=1, replica_groups=mesh['groups'=2,'tp'=16,'tq'=4,'tr'=2] {'tr'}, dimensions={0} | all-to-all | bytes 131072 | tf_op jit(solution)/shard_map/all_to_all | solution.py:25
  121.3 0.0 copy-done.3
  121.3 0.1 fusion.6
  121.4 0.0 copy-start.2
  121.4 27.3 %all-gather.3 = f32[16,2,64]{2,1,0:T(2,128)S(1)} all-gather(f32[1,2,64]{2,1,0:T(2,128)S(1)} %maximum_bitcast_fusion), channel_id=2, replica_groups=mesh['groups'=2,'tp'=16,'tq'=4,'tr'=2] {'tp'}, dimensions={0}, use_global_device_ids=true | all-gather | bytes 8704 | tf_op jit(solution)/shard_map/all_gather | solution.py:37
  148.7 8.5 %all-gather.4 = f32[4,2,64]{2,1,0:T(2,128)S(1)} all-gather(f32[1,2,64]{2,1,0:T(2,128)S(1)} %maximum_bitcast_fusion.1), channel_id=3, replica_groups=mesh['groups'=2,'tp'=16,'tq'=4,'tr'=2] {'tq'}, dimensions={0}, use_global_device_ids=true | all-gather | bytes 2560 | tf_op jit(solution)/shard_map/all_gather | solution.py:37
  157.3 1.9 all-gather.5
  159.1 0.0 copy-start.4
  159.1 0.1 fusion.5
  159.2 3.8 %all_to_all.30 = bf16[2,64,128]{2,1,0:T(8,128)(2,1)S(1)} all-to-all(bf16[2,64,128]{2,1,0:T(8,128)(2,1)S(1)} %broadcast_in_dim.4), channel_id=1, replica_groups=mesh['groups'=2,'tp'=16,'tq'=4,'tr'=2] {'tr'}, dimensions={0} | all-to-all | bytes 65536 | tf_op jit(solution)/shard_map/all_to_all | solution.py:63
  163.0 8.1 %all_to_all.31 = bf16[4,64,256]{2,1,0:T(8,128)(2,1)S(1)} all-to-all(bf16[4,64,256]{2,1,0:T(8,128)(2,1)S(1)} %broadcast_in_dim.5), channel_id=1, replica_groups=mesh['groups'=2,'tp'=16,'tq'=4,'tr'=2] {'tq'}, dimensions={0} | all-to-all | bytes 262144 | tf_op jit(solution)/shard_map/all_to_all | solution.py:63
  171.1 0.3 tile.9
  171.4 0.0 copy-start.1
  171.4 105.6 %all_to_all.32 = bf16[64,16,1024]{2,0,1:T(8,128)(2,1)S(1)} all-to-all(bf16[64,16,1024]{2,0,1:T(8,128)(2,1)S(1)} %tile.9), channel_id=1, replica_groups=mesh['groups'=2,'tp'=16,'tq'=4,'tr'=2] {'tp'}, dimensions={1} | all-to-all | bytes 4194304 | tf_op jit(solution)/shard_map/all_to_all | solution.py:12
  277.0 0.2 copy.19
  277.2 0.0 copy-done.2
  277.3 0.0 copy-done.4
  277.3 0.0 copy-done.1
  277.3 1.5 fusion
  (17 shorter events, 0.2 us)
Async XLA Ops:
  7.2 0.7 copy-start
  7.2 98.3 %reduce-scatter.2.cloned.1.call-start = ((), (), s32[]{:S(2)}) async-start(), calls=%async_computation.6 | async-start | bytes 4456448 | tf_op jit(solution)/shard_map/reduce_scatter | solution.py:76
  12.7 99.4 %copy-start.5 = (bf16[128]{0:T(256)(128)(2,1)S(1)}, bf16[128]{0:T(256)(128)(2,1)}, u32[]{:S(2)}) copy-start(bf16[128]{0:T(256)(128)(2,1)} %param.8) | copy-start | bytes 772
  12.7 108.5 %copy-start.3 = (bf16[64,128]{1,0:T(8,128)(2,1)S(1)}, bf16[64,128]{1,0:T(8,128)(2,1)}, u32[]{:S(2)}) copy-start(bf16[64,128]{1,0:T(8,128)(2,1)} %param.6) | copy-start | bytes 49156
  107.1 10.3 %all-to-all-start = ((f32[4,64,256]{2,1,0:T(8,128)}), f32[4,64,256]{2,1,0:T(8,128)S(1)}, u32[]{:S(2)}, u32[]{:S(2)}) async-start(f32[4,64,256]{2,1,0:T(8,128)} %bitcast.46), calls=%async_computation.1 | async-start | bytes 524288 | tf_op jit(solution)/shard_map/all_to_all | solution.py:25
  121.4 155.9 %copy-start.2 = (bf16[64,128]{1,0:T(8,128)(2,1)}, bf16[64,128]{1,0:T(8,128)(2,1)S(1)}, u32[]{:S(2)}) copy-start(bf16[64,128]{1,0:T(8,128)(2,1)S(1)} %get-tuple-element.8) | copy-start | bytes 49156
  159.1 118.1 %copy-start.4 = (f32[64]{0:T(128)}, f32[64]{0:T(128)S(1)}, u32[]{:S(2)}) copy-start(f32[64]{0:T(128)S(1)} %get-tuple-element.6) | copy-start | bytes 772
  171.4 105.9 %copy-start.1 = (bf16[16384,128]{1,0:T(8,128)(2,1)S(1)}, bf16[16384,128]{1,0:T(8,128)(2,1)}, u32[]{:S(2)}) copy-start(bf16[16384,128]{1,0:T(8,128)(2,1)} %param.9) | copy-start | bytes 12582916
Sparse Core Ops, SparseCore 0:
  12.9 92.5 reduce-scatter.1
